TPU v7x, 32 devices: a whole 2x2x4 slice. The times are simulated.
32 devices in a mesh: dp: 2 (over core), seq: 8 (over z, y), head: 2 (over x).
Axes of the slice: x: 2, y: 2, z: 4, core: 2. Of those that a mesh axis runs over, the one named last changes fastest.
Arguments:
- hidden_in: bfloat16 [8, 1024, 1536], P('dp', 'seq'), may hold values from -6 to 6
- segment_ids: int32 [8, 1024], P('dp', 'seq'), may hold values from 0 to 6, as said below
- position_ids: int32 [8, 1024], P('dp', 'seq'), may hold values from 0 to 1017, as said below
- out_cot: bfloat16 [8, 1024, 1536], P('dp', 'seq'), may hold values from -6 to 6
- attn_gain: bfloat16 [1536], replicated, may hold values from 0.5 to 1.5
- w_query: bfloat16 [1536, 1536], P(('dp', 'seq'), 'head'), may hold values from -0.15625 to 0.15625
- b_query: bfloat16 [12, 128], P('head'), may hold values from -3 to 3
- w_key: bfloat16 [1536, 256], P(('dp', 'seq'), 'head'), may hold values from -0.15625 to 0.15625
- b_key: bfloat16 [2, 128], P('head'), may hold values from -3 to 3
- w_value: bfloat16 [1536, 256], P(('dp', 'seq'), 'head'), may hold values from -0.15625 to 0.15625
- b_value: bfloat16 [2, 128], P('head'), may hold values from -3 to 3
- w_out: bfloat16 [1536, 1536], P('head', ('dp', 'seq')), may hold values from -0.625 to 0.625
- ffn_gain: bfloat16 [1536], replicated, may hold values from 0.5 to 1.5
- w_gate: bfloat16 [1536, 8960], P(('dp', 'seq'), 'head'), may hold values from -0.15625 to 0.15625
- w_up: bfloat16 [1536, 8960], P(('dp', 'seq'), 'head'), may hold values from -0.15625 to 0.15625
- w_down: bfloat16 [8960, 1536], P('head', ('dp', 'seq')), may hold values from -0.125 to 0.125
Outputs:
- layer_out: bfloat16 [8, 1024, 1536], P('dp', 'seq')
- input_grad: bfloat16 [8, 1024, 1536], P('dp', 'seq')
- grad_attn_gain: float32 [1536], P(('dp', 'seq'))
- grad_w_query: float32 [1536, 1536], P(('dp', 'seq'), 'head')
- grad_b_query: float32 [12, 128], P('head', ('dp', 'seq'))
- grad_w_key: float32 [1536, 256], P(('dp', 'seq'), 'head')
- grad_b_key: float32 [2, 128], P('head')
- grad_w_value: float32 [1536, 256], P(('dp', 'seq'), 'head')
- grad_b_value: float32 [2, 128], P('head', ('dp', 'seq'))
- grad_w_out: float32 [1536, 1536], P('head', ('dp', 'seq'))
- grad_ffn_gain: float32 [1536], P(('dp', 'seq'))
- grad_w_gate: float32 [1536, 8960], P(('dp', 'seq'), 'head')
- grad_w_up: float32 [1536, 8960], P(('dp', 'seq'), 'head')
- grad_w_down: float32 [8960, 1536], P('head', ('dp', 'seq'))
Inputs may be any that keep to these rules, and one draw needn't show every extreme that they name: `segment_ids`: each row's 1024 positions are stored in blocks of 128: block number b holds the row's natural positions b * 64 to b * 64 + 63, then 1024 - (b + 1) * 64 to 1024 - b * 64 - 1, each in rising order. In natural order a row holds 6 documents of uneven lengths with ids 1 to 6, rising, then one or more padding positions with id 0. `position_ids`: in natural order (stored as for segment_ids) the ids count 0, 1, 2 and so on from the start of each document and of the padding.
All inputs are finite; a program needn't handle non-finite values.
Results may differ from a plain program's by a relative error of at most 0.024.
Values may be sent and summed in bfloat16 or wider, within the bound.
A program may use at most 256 MiB of HBM per device.

v0:
```python
import math
import jax
import jax.numpy as jnp
from jax import lax
from jax.sharding import PartitionSpec as P

EPSILON = 1e-06
THETA = 1000000.0
MASKED = -1e30


def rope_tables(position, head_size):
    half_size = head_size // 2
    frequency = THETA ** (-jnp.arange(half_size, dtype=jnp.float32) * 2.0 / head_size)
    angles = position.astype(jnp.float32)[:, None] * frequency[None, :]
    return (jnp.cos(angles)[:, None, :], jnp.sin(angles)[:, None, :])


def rotate(values, cosine, sine_table, direction):
    half_size = values.shape[-1] // 2
    first_half = values[..., :half_size]
    second_half = values[..., half_size:]
    return jnp.concatenate(
        [
            first_half * cosine - direction * (second_half * sine_table),
            second_half * cosine + direction * (first_half * sine_table),
        ],
        axis=-1,
    )


def plain_dot(left, right):
    return jnp.dot(left, right, preferred_element_type=jnp.float32)


def grad_of_weight(left, right):
    return lax.dot_general(
        left, right, (((0,), (0,)), ((), ())), preferred_element_type=jnp.float32
    )


def through_weight(left, right):
    return lax.dot_general(
        left, right, (((1,), (1,)), ((), ())), preferred_element_type=jnp.float32
    )


def norm_scale(values):
    return lax.rsqrt(jnp.mean(values * values, axis=-1, keepdims=True) + EPSILON)


def norm_back(grad_in, values, scale_rows, gain):
    scaled = grad_in * gain
    cubed = scale_rows * scale_rows * scale_rows
    return scale_rows * scaled - values * cubed * jnp.mean(scaled * values, axis=-1, keepdims=True)


def block_scores(queries, key_block, key_marks, own_marks, factor):
    scores = (
        jnp.einsum("rqgd,rtd->rgqt", queries, key_block, preferred_element_type=jnp.float32)
        * factor
    )
    allowed = (own_marks[0][:, :, None] == key_marks[0][:, None, :]) & (
        key_marks[1][:, None, :] <= own_marks[1][:, :, None]
    )
    return (scores, allowed[:, None, :, :])


def on_device(
    hidden_in,
    segment_ids,
    position_ids,
    out_cot,
    attn_gain,
    w_query,
    b_query,
    w_key,
    b_key,
    w_value,
    b_value,
    w_out,
    ffn_gain,
    w_gate,
    w_up,
    w_down,
):
    row_count, row_width, model_width = hidden_in.shape
    tokens = row_count * row_width
    groups, head_size = b_query.shape
    factor = head_size ** (-0.5)
    full_query, full_key, full_value, full_gate, full_up, full_out, full_down = (
        lax.all_gather(w_query, ("dp", "seq"), axis=0, tiled=True),
        lax.all_gather(w_key, ("dp", "seq"), axis=0, tiled=True),
        lax.all_gather(w_value, ("dp", "seq"), axis=0, tiled=True),
        lax.all_gather(w_gate, ("dp", "seq"), axis=0, tiled=True),
        lax.all_gather(w_up, ("dp", "seq"), axis=0, tiled=True),
        lax.all_gather(w_out, ("dp", "seq"), axis=1, tiled=True),
        lax.all_gather(w_down, ("dp", "seq"), axis=1, tiled=True),
    )
    own_marks = jnp.stack([segment_ids, position_ids])
    key_labels = lax.all_gather(own_marks, "seq", axis=2, tiled=True)
    length = key_labels.shape[2]
    key_rows = math.gcd(length, 512)
    block_count = length // key_rows
    hidden = hidden_in.reshape(tokens, model_width).astype(jnp.float32)
    scale_one = norm_scale(hidden)
    gain_one = attn_gain.astype(jnp.float32)
    normed = (hidden * scale_one * gain_one).astype(jnp.bfloat16)
    cosine, sine_table = rope_tables(position_ids.reshape(tokens), head_size)
    query_pre = plain_dot(normed, full_query) + b_query.reshape(-1).astype(jnp.float32)
    key_pre = plain_dot(normed, full_key) + b_key.reshape(-1).astype(jnp.float32)
    value_pre = plain_dot(normed, full_value) + b_value.reshape(-1).astype(jnp.float32)
    queries = rotate(query_pre.reshape(tokens, groups, head_size), cosine, sine_table, 1.0).astype(
        jnp.bfloat16
    )
    queries = queries.reshape(row_count, row_width, groups, head_size)
    key_rot = rotate(key_pre.reshape(tokens, 1, head_size), cosine, sine_table, 1.0).astype(
        jnp.bfloat16
    )
    local_kv = jnp.concatenate(
        [key_rot.reshape(tokens, head_size), value_pre.astype(jnp.bfloat16)], axis=-1
    )
    all_kv = lax.all_gather(
        local_kv.reshape(row_count, row_width, 2 * head_size), "seq", axis=1, tiled=True
    )

    def key_slices(step_index):
        offset = step_index * key_rows
        kv_block = lax.dynamic_slice_in_dim(all_kv, offset, key_rows, 1)
        key_marks = lax.dynamic_slice_in_dim(key_labels, offset, key_rows, 2)
        scores, allowed = block_scores(
            queries, kv_block[..., :head_size], key_marks, own_marks, factor
        )
        return (offset, kv_block, scores, allowed)

    def max_step(step_index, state_pair):
        running_max, running_sum = state_pair
        offset, kv_block, scores, allowed = key_slices(step_index)
        masked = jnp.where(allowed, scores, MASKED)
        fresh_max = jnp.maximum(running_max, jnp.max(masked, axis=-1))
        exp_terms = jnp.where(allowed, jnp.exp(masked - fresh_max[..., None]), 0.0)
        return (
            fresh_max,
            running_sum * jnp.exp(running_max - fresh_max) + jnp.sum(exp_terms, axis=-1),
        )

    stat_shape = (row_count, groups, row_width)
    running_max, running_sum = lax.fori_loop(
        0,
        block_count,
        max_step,
        (jnp.full(stat_shape, MASKED, jnp.float32), jnp.zeros(stat_shape, jnp.float32)),
    )
    log_total = running_max + jnp.log(running_sum)

    def block_probs(scores, allowed):
        return jnp.where(allowed, jnp.exp(scores - log_total[..., None]), 0.0)

    def output_step(step_index, accum):
        offset, kv_block, scores, allowed = key_slices(step_index)
        weights = block_probs(scores, allowed).astype(jnp.bfloat16)
        return accum + jnp.einsum(
            "rgqt,rtd->rqgd", weights, kv_block[..., head_size:], preferred_element_type=jnp.float32
        )

    attended = lax.fori_loop(
        0,
        block_count,
        output_step,
        jnp.zeros((row_count, row_width, groups, head_size), jnp.float32),
    )
    mixed = attended.reshape(tokens, groups * head_size).astype(jnp.bfloat16)
    middle = hidden + lax.psum(plain_dot(mixed, full_out), "head")
    scale_two = norm_scale(middle)
    gain_two = ffn_gain.astype(jnp.float32)
    normed_two = (middle * scale_two * gain_two).astype(jnp.bfloat16)
    gate_pre = plain_dot(normed_two, full_gate)
    up_pre = plain_dot(normed_two, full_up)
    sigmoid_gate = jax.nn.sigmoid(gate_pre)
    activated = gate_pre * sigmoid_gate
    product = (activated * up_pre).astype(jnp.bfloat16)
    result = middle + lax.psum(plain_dot(product, full_down).astype(jnp.bfloat16), "head").astype(
        jnp.float32
    )
    layer_out = result.astype(jnp.bfloat16).reshape(row_count, row_width, model_width)
    live_rows = (segment_ids != 0).astype(jnp.float32).reshape(tokens, 1)
    cotangent = out_cot.reshape(tokens, model_width).astype(jnp.float32) * live_rows
    cot_low = cotangent.astype(jnp.bfloat16)
    full_query, full_key, full_value, full_gate, full_up, full_out, full_down = (
        lax.all_gather(w_query, ("dp", "seq"), axis=0, tiled=True),
        lax.all_gather(w_key, ("dp", "seq"), axis=0, tiled=True),
        lax.all_gather(w_value, ("dp", "seq"), axis=0, tiled=True),
        lax.all_gather(w_gate, ("dp", "seq"), axis=0, tiled=True),
        lax.all_gather(w_up, ("dp", "seq"), axis=0, tiled=True),
        lax.all_gather(w_out, ("dp", "seq"), axis=1, tiled=True),
        lax.all_gather(w_down, ("dp", "seq"), axis=1, tiled=True),
    )
    grad_down_w = grad_of_weight(product, cot_low)
    d_product = through_weight(cot_low, full_down).astype(jnp.bfloat16).astype(jnp.float32)
    d_gate = (d_product * up_pre * sigmoid_gate * (1.0 + gate_pre * (1.0 - sigmoid_gate))).astype(
        jnp.bfloat16
    )
    d_up = (d_product * activated).astype(jnp.bfloat16)
    grad_gate_w = grad_of_weight(normed_two, d_gate)
    grad_up_w = grad_of_weight(normed_two, d_up)
    back_two = lax.psum(through_weight(d_gate, full_gate) + through_weight(d_up, full_up), "head")
    gain_two_grad = jnp.sum(back_two * middle * scale_two, axis=0)
    gate_sum, up_sum, down_sum, gain_two_sum = (grad_gate_w, grad_up_w, grad_down_w, gain_two_grad)
    d_middle = cotangent + norm_back(back_two, middle, scale_two, gain_two)
    d_middle_low = d_middle.astype(jnp.bfloat16)
    grad_out_w = grad_of_weight(mixed, d_middle_low)
    d_mixed = (
        through_weight(d_middle_low, full_out)
        .astype(jnp.bfloat16)
        .reshape(row_count, row_width, groups, head_size)
    )

    def delta_step(step_index, row_delta):
        offset, kv_block, scores, allowed = key_slices(step_index)
        probs = block_probs(scores, allowed)
        d_probs = jnp.einsum(
            "rqgd,rtd->rgqt", d_mixed, kv_block[..., head_size:], preferred_element_type=jnp.float32
        )
        return row_delta + jnp.sum(probs * d_probs, axis=-1)

    row_delta = lax.fori_loop(0, block_count, delta_step, jnp.zeros(stat_shape, jnp.float32))

    def grad_step(step_index, state_pair):
        query_accum, kv_buffer = state_pair
        offset, kv_block, scores, allowed = key_slices(step_index)
        probs = block_probs(scores, allowed)
        weights = probs.astype(jnp.bfloat16)
        d_probs = jnp.einsum(
            "rqgd,rtd->rgqt", d_mixed, kv_block[..., head_size:], preferred_element_type=jnp.float32
        )
        d_scores = (probs * (d_probs - row_delta[..., None])).astype(jnp.bfloat16)
        query_accum = query_accum + jnp.einsum(
            "rgqt,rtd->rqgd",
            d_scores,
            kv_block[..., :head_size],
            preferred_element_type=jnp.float32,
        )
        key_terms = jnp.einsum(
            "rgqt,rqgd->rtd", d_scores, queries, preferred_element_type=jnp.float32
        )
        value_terms = jnp.einsum(
            "rgqt,rqgd->rtd", weights, d_mixed, preferred_element_type=jnp.float32
        )
        kv_buffer = lax.dynamic_update_slice_in_dim(
            kv_buffer, jnp.concatenate([key_terms, value_terms], axis=-1), offset, 1
        )
        return (query_accum, kv_buffer)

    query_accum, kv_buffer = lax.fori_loop(
        0,
        block_count,
        grad_step,
        (
            jnp.zeros((row_count, row_width, groups, head_size), jnp.float32),
            jnp.zeros((row_count, length, 2 * head_size), jnp.float32),
        ),
    )
    d_kv = lax.psum_scatter(kv_buffer, "seq", scatter_dimension=1, tiled=True).reshape(
        tokens, 2 * head_size
    )
    d_key = (
        rotate(
            (d_kv[:, :head_size] * factor).reshape(tokens, 1, head_size), cosine, sine_table, -1.0
        )
        .reshape(tokens, head_size)
        .astype(jnp.bfloat16)
    )
    d_value = d_kv[:, head_size:].astype(jnp.bfloat16)
    d_query = (
        rotate(query_accum.reshape(tokens, groups, head_size) * factor, cosine, sine_table, -1.0)
        .reshape(tokens, groups * head_size)
        .astype(jnp.bfloat16)
    )
    replicas = lax.axis_size(("dp", "seq"))
    bias_query = jnp.sum(d_query.astype(jnp.float32), axis=0).reshape(groups, head_size)
    bias_key = jnp.sum(d_key.astype(jnp.float32), axis=0).reshape(1, head_size)
    bias_key_wide = jnp.tile(bias_key, (1, replicas))
    bias_value = jnp.sum(d_value.astype(jnp.float32), axis=0).reshape(1, head_size)
    grad_query_w = grad_of_weight(normed, d_query)
    grad_key_w = grad_of_weight(normed, d_key)
    grad_value_w = grad_of_weight(normed, d_value)
    back_one = (
        through_weight(d_query, full_query)
        + through_weight(d_key, full_key)
        + through_weight(d_value, full_value)
    )
    back_one = lax.psum(back_one.astype(jnp.bfloat16), "head").astype(jnp.float32)
    gain_one_grad = jnp.sum(back_one * hidden * scale_one, axis=0)
    d_hidden = d_middle + norm_back(back_one, hidden, scale_one, gain_one)
    input_grad = d_hidden.astype(jnp.bfloat16).reshape(row_count, row_width, model_width)
    (
        query_sum,
        key_sum,
        value_sum,
        out_sum,
        gain_one_sum,
        bq_sum,
        bk_sum,
        bv_sum,
        gate_sum,
        up_sum,
        down_sum,
        gain_two_sum,
    ) = (
        lax.psum_scatter(grad_query_w, ("dp", "seq"), scatter_dimension=0, tiled=True),
        lax.psum_scatter(grad_key_w, ("dp", "seq"), scatter_dimension=0, tiled=True),
        lax.psum_scatter(grad_value_w, ("dp", "seq"), scatter_dimension=0, tiled=True),
        lax.psum_scatter(grad_out_w, ("dp", "seq"), scatter_dimension=1, tiled=True),
        lax.psum_scatter(gain_one_grad, ("dp", "seq"), scatter_dimension=0, tiled=True),
        lax.psum_scatter(bias_query, ("dp", "seq"), scatter_dimension=1, tiled=True),
        lax.psum_scatter(bias_key_wide, ("dp", "seq"), scatter_dimension=1, tiled=True),
        lax.psum_scatter(bias_value, ("dp", "seq"), scatter_dimension=1, tiled=True),
        lax.psum_scatter(gate_sum, ("dp", "seq"), scatter_dimension=0, tiled=True),
        lax.psum_scatter(up_sum, ("dp", "seq"), scatter_dimension=0, tiled=True),
        lax.psum_scatter(down_sum, ("dp", "seq"), scatter_dimension=1, tiled=True),
        lax.psum_scatter(gain_two_sum, ("dp", "seq"), scatter_dimension=0, tiled=True),
    )
    return (
        layer_out,
        input_grad,
        gain_one_sum,
        query_sum,
        bq_sum,
        key_sum,
        bk_sum,
        value_sum,
        bv_sum,
        out_sum,
        gain_two_sum,
        gate_sum,
        up_sum,
        down_sum,
    )


def solution(mesh):
    placed = (
        P("dp", "seq", None),
        P("dp", "seq"),
        P("dp", "seq"),
        P("dp", "seq", None),
        P(),
        P(("dp", "seq"), "head"),
        P("head", None),
        P(("dp", "seq"), "head"),
        P("head", None),
        P(("dp", "seq"), "head"),
        P("head", None),
        P("head", ("dp", "seq")),
        P(),
        P(("dp", "seq"), "head"),
        P(("dp", "seq"), "head"),
        P("head", ("dp", "seq")),
    )
    return jax.shard_map(
        on_device,
        mesh=mesh,
        in_specs=placed,
        out_specs=(
            P("dp", "seq", None),
            P("dp", "seq", None),
            P(("dp", "seq")),
            P(("dp", "seq"), "head"),
            P("head", ("dp", "seq")),
            P(("dp", "seq"), "head"),
            P("head", None),
            P(("dp", "seq"), "head"),
            P("head", ("dp", "seq")),
            P("head", ("dp", "seq")),
            P(("dp", "seq")),
            P(("dp", "seq"), "head"),
            P(("dp", "seq"), "head"),
            P("head", ("dp", "seq")),
        ),
        check_vma=False,
    )
```

profile of v0, /device:TPU:0, one launch (start us, length us, event | category | flops | bytes accessed | tf_op | source)
XLA Modules:
  0.0 2139.3 jit_solution(3503738205872189389)
XLA Ops:
  8.7 38.7 %all_gather.34 = bf16[1536,128]{1,0:T(8,128)(2,1)S(1)} all-gather(bf16[96,128]{1,0:T(8,128)(2,1)} %param.31), channel_id=1, replica_groups=mesh['dp'=2,'seq'=8,'head'=2] {'dp','seq'}, dimensions={0}, use_global_device_ids=true | all-gather | bytes 417792 | tf_op jit(solution)/shard_map/all_gather | solution.py:93
  53.2 30.5 %all_gather.35 = bf16[1536,128]{1,0:T(8,128)(2,1)S(1)} all-gather(bf16[96,128]{1,0:T(8,128)(2,1)S(1)} %copy-done.46), channel_id=1, replica_groups=mesh['dp'=2,'seq'=8,'head'=2] {'dp','seq'}, dimensions={0}, use_global_device_ids=true | all-gather | bytes 417792 | tf_op jit(solution)/shard_map/all_gather | solution.py:94
  88.3 26.5 %all_gather.37 = s32[2,4,1024]{2,1,0:T(4,128)S(1)} all-gather(s32[2,4,128]{2,1,0:T(4,128)S(1)} %pad_add_fusion), channel_id=1, replica_groups=mesh['dp'=2,'seq'=8,'head'=2] {'seq'}, dimensions={2}, use_global_device_ids=true | all-gather | bytes 36864 | tf_op jit(solution)/shard_map/all_gather | solution.py:101
  125.2 10.0 all-gather.7.cloned.1.call-done
  135.3 19.7 while.60
  136.0 4.7 fusion.176
  145.9 4.7 fusion.176
  155.0 10.3 while.61
  160.5 4.8 bitcast_add_fusion.6
  167.5 10.9 all-gather.11.cloned.1.call-done
  178.4 4.8 fusion.70
  188.1 79.8 %all-reduce.10.cloned.1.call-done = f32[512,1536]{1,0:T(8,128)} async-done(((f32[512,1536]{1,0:T(8,128)}), f32[512,1536]{1,0:T(8,128)}) %all-reduce.10.cloned.1.call-update) | async-done | bytes 3145744 | tf_op jit(solution)/shard_map/psum | solution.py:173
  273.4 104.3 %all-gather.17.cloned.1.call-done = bf16[4480,1536]{0,1:T(8,128)(2,1)} async-done(((bf16[4480,96]{0,1:T(8,128)(2,1)}), bf16[4480,1536]{0,1:T(8,128)(2,1)}) %all-gather.17.cloned.1.call-update) | async-done | bytes 13762576 | tf_op jit(solution)/shard_map/all_gather | solution.py:98
  377.7 14.3 convolution_convert_fusion
  392.0 93.7 %all-gather.13.cloned.1.call-done = bf16[1536,4480]{1,0:T(8,128)(2,1)} async-done(((bf16[96,4480]{1,0:T(8,128)(2,1)}), bf16[1536,4480]{1,0:T(8,128)(2,1)}) %all-gather.13.cloned.1.call-update) | async-done | bytes 13762576 | tf_op jit(solution)/shard_map/all_gather | solution.py:95
  485.7 13.2 fusion.107
  498.8 95.0 %all-gather.15.cloned.1.call-done = bf16[1536,4480]{1,0:T(8,128)(2,1)} async-done(((bf16[96,4480]{1,0:T(8,128)(2,1)}), bf16[1536,4480]{1,0:T(8,128)(2,1)}) %all-gather.15.cloned.1.call-update) | async-done | bytes 13762576 | tf_op jit(solution)/shard_map/all_gather | solution.py:96
  593.8 17.7 fusion.46
  613.6 12.0 fusion.108
  625.6 19.2 convolution_add_fusion.2
  646.4 82.6 %all-reduce.12.cloned.1.call-done = f32[512,1536]{1,0:T(8,128)} async-done(((f32[512,1536]{1,0:T(8,128)}), f32[512,1536]{1,0:T(8,128)}) %all-reduce.12.cloned.1.call-update) | async-done | bytes 3145744 | tf_op jit(solution)/shard_map/psum | solution.py:206
  729.0 4.4 multiply_reduce_fusion
  740.1 20.2 while.62
  740.1 4.6 fusion.182
  745.4 4.7 fusion.183
  750.2 4.6 fusion.182
  755.5 4.7 fusion.183
  762.7 43.6 %while.63 = (s32[]{:T(128)}, f32[4,128,6,128]{1,3,2,0:T(8,128)}, f32[4,1024,256]{1,2,0:T(8,128)}, bf16[4,1024,256]{2,1,0:T(8,128)(2,1)}, s32[4,128]{1,0:T(4,128)...) while((s32[]{:T(128)}, f32[4,128,6,128]{1,3,2,0:T(8,128)}, ...), condition=%wide.region_16.17_spmd.clone, body=%wide.region_15.16_spmd.clone.sunk | while | flops 2031091712 | bytes 111866424 | solution.py:254
  762.8 4.9 fusion.191
  768.4 5.1 fusion.192
  784.3 4.9 fusion.191
  790.0 5.1 fusion.192
  806.4 13.2 convolution_convert_fusion.1
  827.7 67.5 %reduce-scatter.14.cloned.1.call-done = f32[4,128,256]{1,2,0:T(8,128)} async-done(((f32[4,1024,256]{1,2,0:T(8,128)}), f32[4,128,256]{1,2,0:T(8,128)}) %reduce-scatter.14.cloned.1.call-update) | async-done | bytes 524304 | tf_op jit(solution)/shard_map/reduce_scatter | solution.py:263
  913.9 4.7 fusion.68
  924.3 15.1 fusion.111
  939.5 18.1 fusion.103
  959.0 15.1 fusion.112
  978.1 69.3 %all-reduce.14.cloned.1.call-done = (bf16[512,1536]{1,0:T(8,128)(2,1)}, bf16[512,1536]{1,0:T(8,128)(2,1)}) async-done(((bf16[512,1536]{1,0:T(8,128)(2,1)}, bf16[512,1536]{1,0:T(8,128)(2,1)}), (bf16[512,1536]{1,0:T(8,128)(2,1)}, bf16[512,1536]{1,0:T(8,128)(2,1)})) %all-reduce.14.cloned.1.call-update) | async-done | bytes 3145744 | tf_op jit(solution)/shard_map/psum | solution.py:182
  1050.6 62.7 %all-reduce.4 = (f32[1536]{0:T(1024)S(1)}, f32[6,128]{1,0:T(8,128)S(1)}, f32[1,128]{1,0:T(1,128)S(1)}, f32[1536]{0:T(1024)S(1)}) all-reduce(f32[1536]{0:T(1024)S(1)} %get-tuple-element.868, f32[6,128]{1,0:T(8,128)S(1)} %get-tuple-element.948, ...), channel_id=3, replica_groups=mesh['dp'=2,'seq'=8,'head'=2] {'dp','seq'}, use_global_device_ids=true, to_apply=%region_21.22.clone | all-reduce | flops 3968 | bytes 31744
  1115.7 5.1 fusion.53
  1120.8 7.3 reduce-scatter.16.cloned.1.call-done
  1128.1 79.2 %reduce-scatter.22.cloned.1.call-done = f32[768,96]{0,1:T(8,128)} async-done(((f32[768,1536]{0,1:T(8,128)}), f32[768,96]{0,1:T(8,128)}) %reduce-scatter.22.cloned.1.call-update) | async-done | bytes 294928 | tf_op jit(solution)/shard_map/reduce_scatter | solution.py:313
  1207.3 59.9 %reduce-scatter.18.cloned.1.call-done = f32[96,128]{1,0:T(8,128)} async-done(((f32[1536,128]{1,0:T(8,128)}), f32[96,128]{1,0:T(8,128)}) %reduce-scatter.18.cloned.1.call-update) | async-done | bytes 49168 | tf_op jit(solution)/shard_map/reduce_scatter | solution.py:311
  1267.2 59.8 %reduce-scatter.20.cloned.1.call-done = f32[96,128]{1,0:T(8,128)} async-done(((f32[1536,128]{1,0:T(8,128)}), f32[96,128]{1,0:T(8,128)}) %reduce-scatter.20.cloned.1.call-update) | async-done | bytes 49168 | tf_op jit(solution)/shard_map/reduce_scatter | solution.py:312
  1327.0 268.3 %reduce-scatter.24.cloned.1.call-done = f32[96,4480]{1,0:T(8,128)} async-done(((f32[1536,4480]{1,0:T(8,128)}), f32[96,4480]{1,0:T(8,128)}) %reduce-scatter.24.cloned.1.call-update) | async-done | bytes 1720336 | tf_op jit(solution)/shard_map/reduce_scatter | solution.py:318
  1595.2 268.4 %reduce-scatter.26.cloned.1.call-done = f32[96,4480]{1,0:T(8,128)} async-done(((f32[1536,4480]{1,0:T(8,128)}), f32[96,4480]{1,0:T(8,128)}) %reduce-scatter.26.cloned.1.call-update) | async-done | bytes 1720336 | tf_op jit(solution)/shard_map/reduce_scatter | solution.py:319
  1863.6 268.4 %reduce-scatter.28.cloned.1.call-done = f32[4480,96]{0,1:T(8,128)} async-done(((f32[4480,1536]{0,1:T(8,128)}), f32[4480,96]{0,1:T(8,128)}) %reduce-scatter.28.cloned.1.call-update) | async-done | bytes 1720336 | tf_op jit(solution)/shard_map/reduce_scatter | solution.py:320
  (292 shorter events, 129.3 us)
Async XLA Ops:
  7.2 43.4 %copy-start.7 = (bf16[4,128,1536]{2,1,0:T(8,128)(2,1)S(1)}, bf16[4,128,1536]{2,1,0:T(8,128)(2,1)}, u32[]{:S(2)}) copy-start(bf16[4,128,1536]{2,1,0:T(8,128)(2,1)} %param.24) | copy-start | bytes 4718596
  7.2 107.6 %all-gather.9.cloned.1.call-start = ((), (), s32[]{:S(2)}) async-start(), calls=%async_computation.10 | async-start | bytes 2506752 | tf_op jit(solution)/shard_map/all_gather | solution.py:92
  7.9 127.3 %all-gather.7.cloned.1.call-start = ((), (), s32[]{:S(2)}) async-start(), calls=%async_computation.9 | async-start | bytes 2359296 | tf_op jit(solution)/shard_map/all_gather | solution.py:123
  8.7 43.1 %copy-start.39 = (f32[1536]{0:T(1024)}, f32[1536]{0:T(1024)S(1)}, u32[]{:S(2)}) copy-start(f32[1536]{0:T(1024)S(1)} %convert_element_type.175) | copy-start | bytes 18436
  8.7 79.0 %copy-start.52 = (f32[64]{0:T(128)}, f32[64]{0:T(128)S(1)}, u32[]{:S(2)}) copy-start(f32[64]{0:T(128)S(1)} %multiply_power_fusion) | copy-start | bytes 772
  49.3 34.4 %copy-start.47 = (f32[4,128]{1,0:T(4,128)}, f32[4,128]{1,0:T(4,128)S(1)}, u32[]{:S(2)}) copy-start(f32[4,128]{1,0:T(4,128)S(1)} %fusion.59) | copy-start | bytes 6148
  50.6 33.1 %copy-start.58 = (bf16[1,128]{1,0:T(2,128)(2,1)S(1)}, bf16[1,128]{1,0:T(2,128)(2,1)}, u32[]{:S(2)}) copy-start(bf16[1,128]{1,0:T(2,128)(2,1)} %param.34) | copy-start | bytes 772
  51.0 63.8 %copy-start.11 = (bf16[512,1536]{1,0:T(8,128)(2,1)}, bf16[512,1536]{1,0:T(8,128)(2,1)S(1)}, u32[]{:S(2)}) copy-start(bf16[512,1536]{1,0:T(8,128)(2,1)S(1)} %fusion.63) | copy-start | bytes 4718596
  51.0 37.2 %copy-start.37 = (s32[4,128]{1,0:T(4,128)S(1)}, s32[4,128]{1,0:T(4,128)}, u32[]{:S(2)}) copy-start(s32[4,128]{1,0:T(4,128)} %param.25) | copy-start | bytes 6148
  51.0 63.7 %copy-start.55 = (bf16[6,128]{1,0:T(8,128)(2,1)S(1)}, bf16[6,128]{1,0:T(8,128)(2,1)}, u32[]{:S(2)}) copy-start(bf16[6,128]{1,0:T(8,128)(2,1)} %param.30) | copy-start | bytes 4612
  51.8 36.4 %copy-start.41 = (f32[512]{0:T(512)}, f32[512]{0:T(512)S(1)}, u32[]{:S(2)}) copy-start(f32[512]{0:T(512)S(1)} %convert_bitcast_fusion.1) | copy-start | bytes 6148
  86.8 91.5 %all-gather.11.cloned.1.call-start = ((), (), s32[]{:S(2)}) async-start(), calls=%async_computation.11 | async-start | bytes 2506752 | tf_op jit(solution)/shard_map/all_gather | solution.py:97
  87.6 180.3 %all-reduce.10.cloned.1.call-start = ((), (), s32[]{:S(2)}) async-start(), calls=%async_computation.12 | async-start | bytes 6291456 | tf_op jit(solution)/shard_map/psum | solution.py:173
  88.2 32.7 %copy-start.32 = (f32[512,64]{0,1:T(8,128)}, f32[512,64]{0,1:T(8,128)S(1)}, u32[]{:S(2)}) copy-start(f32[512,64]{0,1:T(8,128)S(1)} %get-tuple-element.976) | copy-start | bytes 393220
  88.2 32.7 %copy-start.34 = (f32[512,64]{0,1:T(8,128)}, f32[512,64]{0,1:T(8,128)S(1)}, u32[]{:S(2)}) copy-start(f32[512,64]{0,1:T(8,128)S(1)} %get-tuple-element.977) | copy-start | bytes 393220
  124.5 10.7 copy-start.19
  167.5 15.7 copy-start.20
  183.2 194.5 %all-gather.17.cloned.1.call-start = ((), (), s32[]{:S(2)}) async-start(), calls=%async_computation.15 | async-start | bytes 14622720 | tf_op jit(solution)/shard_map/all_gather | solution.py:98
  183.8 301.9 %all-gather.13.cloned.1.call-start = ((), (), s32[]{:S(2)}) async-start(), calls=%async_computation.13 | async-start | bytes 14622720 | tf_op jit(solution)/shard_map/all_gather | solution.py:95
  184.4 409.5 %all-gather.15.cloned.1.call-start = ((), (), s32[]{:S(2)}) async-start(), calls=%async_computation.14 | async-start | bytes 14622720 | tf_op jit(solution)/shard_map/all_gather | solution.py:96
  185.1 543.9 %all-reduce.12.cloned.1.call-start = ((), (), s32[]{:S(2)}) async-start(), calls=%async_computation.16 | async-start | bytes 6291456 | tf_op jit(solution)/shard_map/psum | solution.py:206
  270.3 107.4 %copy-start.28 = (bf16[512,1536]{1,0:T(8,128)(2,1)S(1)}, bf16[512,1536]{1,0:T(8,128)(2,1)}, u32[]{:S(2)}) copy-start(bf16[512,1536]{1,0:T(8,128)(2,1)} %fusion.58) | copy-start | bytes 4718596
  392.0 201.8 %copy-start.30 = (bf16[512,1536]{1,0:T(8,128)(2,1)S(1)}, bf16[512,1536]{1,0:T(8,128)(2,1)}, u32[]{:S(2)}) copy-start(bf16[512,1536]{1,0:T(8,128)(2,1)} %multiply_convert_fusion.1) | copy-start | bytes 4718596
  644.9 250.3 %reduce-scatter.14.cloned.1.call-start = ((), (), s32[]{:S(2)}) async-start(), calls=%async_computation.17 | async-start | bytes 4718592 | tf_op jit(solution)/shard_map/reduce_scatter | solution.py:263
  644.9 88.5 %copy-start.18 = (bf16[4,128,1536]{2,1,0:T(8,128)(2,1)S(1)}, bf16[4,128,1536]{2,1,0:T(8,128)(2,1)}, u32[]{:S(2)}) copy-start(bf16[4,128,1536]{2,1,0:T(8,128)(2,1)} %param.27) | copy-start | bytes 4718596
  762.7 4.9 copy-start.49
  762.7 4.9 copy-start.21
  784.3 4.9 copy-start.1
  784.3 4.9 copy-start.49
  784.3 4.9 copy-start.21
  806.3 170.3 %reduce-scatter.30.cloned.1.call-start = ((), (), s32[]{:S(2)}) async-start(), calls=%async_computation.25 | async-start | bytes 1114112
  806.4 13.2 copy-start.3
  824.5 71.9 %copy-start.42 = (f32[512]{0:T(512)S(1)}, f32[512]{0:T(512)}, u32[]{:S(2)}) copy-start(f32[512]{0:T(512)} %copy-done.41) | copy-start | bytes 6148
  824.5 71.9 %copy-start.53 = (f32[64]{0:T(128)S(1)}, f32[64]{0:T(128)}, u32[]{:S(2)}) copy-start(f32[64]{0:T(128)} %copy-done.52) | copy-start | bytes 772
  824.5 72.6 %copy-start.25 = (bf16[1536,128]{1,0:T(8,128)(2,1)S(1)}, bf16[1536,128]{1,0:T(8,128)(2,1)}, u32[]{:S(2)}) copy-start(bf16[1536,128]{1,0:T(8,128)(2,1)} %copy-done.24) | copy-start | bytes 1179652
  896.3 6.6 copy-start.23
  897.2 5.8 copy-start.27
  902.9 144.6 %all-reduce.14.cloned.1.call-start = ((), (), s32[]{:S(2)}) async-start(), calls=%async_computation.26 | async-start | bytes 6291456 | tf_op jit(solution)/shard_map/psum | solution.py:182
  906.7 221.4 %reduce-scatter.16.cloned.1.call-start = ((), (), s32[]{:S(2)}) async-start(), calls=%async_computation.18 | async-start | bytes 5013504 | tf_op jit(solution)/shard_map/reduce_scatter | solution.py:310
  912.0 295.3 %reduce-scatter.22.cloned.1.call-start = ((), (), s32[]{:S(2)}) async-start(), calls=%async_computation.21 | async-start | bytes 5013504 | tf_op jit(solution)/shard_map/reduce_scatter | solution.py:313
  918.7 348.5 %reduce-scatter.18.cloned.1.call-start = ((), (), s32[]{:S(2)}) async-start(), calls=%async_computation.19 | async-start | bytes 835584 | tf_op jit(solution)/shard_map/reduce_scatter | solution.py:311
  921.6 405.3 %reduce-scatter.20.cloned.1.call-start = ((), (), s32[]{:S(2)}) async-start(), calls=%async_computation.20 | async-start | bytes 835584 | tf_op jit(solution)/shard_map/reduce_scatter | solution.py:312
  924.3 671.0 %reduce-scatter.24.cloned.1.call-start = ((), (), s32[]{:S(2)}) async-start(), calls=%async_computation.22 | async-start | bytes 29245440 | tf_op jit(solution)/shard_map/reduce_scatter | solution.py:318
  939.4 924.2 %reduce-scatter.26.cloned.1.call-start = ((), (), s32[]{:S(2)}) async-start(), calls=%async_computation.23 | async-start | bytes 29245440 | tf_op jit(solution)/shard_map/reduce_scatter | solution.py:319
  957.6 1174.4 %reduce-scatter.28.cloned.1.call-start = ((), (), s32[]{:S(2)}) async-start(), calls=%async_computation.24 | async-start | bytes 29245440 | tf_op jit(solution)/shard_map/reduce_scatter | solution.py:320
  974.1 73.4 %copy-start.45 = (f32[512]{0:T(512)S(1)}, f32[512]{0:T(512)}, u32[]{:S(2)}) copy-start(f32[512]{0:T(512)} %copy-done.44) | copy-start | bytes 6148
  974.1 76.4 %copy-start.43 = (f32[1536]{0:T(1024)S(1)}, f32[1536]{0:T(1024)}, u32[]{:S(2)}) copy-start(f32[1536]{0:T(1024)} %get-tuple-element.866) | copy-start | bytes 18436
  974.2 141.6 %copy-start.6 = (f32[512,1536]{1,0:T(8,128)S(1)}, f32[512,1536]{1,0:T(8,128)}, u32[]{:S(2)}) copy-start(f32[512,1536]{1,0:T(8,128)} %copy-done.4) | copy-start | bytes 9437188
  (41 other events, 108.0 us)
Sparse Core Ops, SparseCore 0:
  10.2 46.0 all-gather.8
  87.0 48.2 all-gather.6
  137.5 40.8 all-gather.10
  183.3 84.5 all-reduce.9
  270.0 107.6 all-gather.16
  379.8 105.8 all-gather.12
  487.9 105.8 all-gather.14
  645.0 83.9 all-reduce.11
  806.5 88.6 reduce-scatter.13
  903.0 57.1 reduce-scatter.29
  962.6 84.8 all-reduce.13
  1051.8 76.2 reduce-scatter.15
  1132.5 74.7 reduce-scatter.21
  1211.3 55.8 reduce-scatter.17
  1271.2 55.7 reduce-scatter.19
  1331.5 263.6 reduce-scatter.23
  1599.8 263.7 reduce-scatter.25
  1868.2 263.7 reduce-scatter.27
where the time goes:
time: 2140 us
  waiting for transfers between devices  1630 us (76%)
  matrix products  246 us (11%)
  blocking collectives  158 us (7%)
  other arithmetic  48.2 us (2%)
  local copies, waits for them, and re-layouts  40.8 us (2%)
    reduce_scatter x1, waiting for transfers between devices, on_device(): lax.psum_scatter(down_sum, ('dp', 'seq'), scatter_dimension=1, tiled=True)  268 us
    reduce_scatter x1, waiting for transfers between devices, on_device(): lax.psum_scatter(up_sum, ('dp', 'seq'), scatter_dimension=0, tiled=True)  268 us
    reduce_scatter x1, waiting for transfers between devices, on_device(): lax.psum_scatter(gate_sum, ('dp', 'seq'), scatter_dimension=0, tiled=True)  268 us
    all_gather x1, waiting for transfers between devices, on_device(): lax.all_gather(w_down, ('dp', 'seq'), axis=1, tiled=True)  104 us
    all_gather x1, waiting for transfers between devices, on_device(): lax.all_gather(w_up, ('dp', 'seq'), axis=0, tiled=True)  95 us
    all_gather x1, waiting for transfers between devices, on_device(): lax.all_gather(w_gate, ('dp', 'seq'), axis=0, tiled=True)  93.7 us
    psum x1, waiting for transfers between devices, on_device(): lax.psum(through_weight(d_gate, full_gate) + through_weight(d_up, full_up...  82.6 us
    psum x1, waiting for transfers between devices, on_device(): middle = hidden + lax.psum(plain_dot(mixed, full_out), 'head')  79.8 us
  transfers between devices with their start and end apart: 18, of which 16 were waited for; matrix products, arithmetic and copies ran while one was open for 9% of the time, Pallas kernels for 0%

commit v1 on v0

--- a/solution.py
+++ b/solution.py
@@ -203,7 +203,10 @@
     d_up = (d_product * activated).astype(jnp.bfloat16)
     grad_gate_w = grad_of_weight(normed_two, d_gate)
     grad_up_w = grad_of_weight(normed_two, d_up)
-    back_two = lax.psum(through_weight(d_gate, full_gate) + through_weight(d_up, full_up), "head")
+    back_two = jnp.sum(
+        lax.all_gather(through_weight(d_gate, full_gate) + through_weight(d_up, full_up), "head"),
+        axis=0,
+    )
     gain_two_grad = jnp.sum(back_two * middle * scale_two, axis=0)
     gate_sum, up_sum, down_sum, gain_two_sum = (grad_gate_w, grad_up_w, grad_down_w, gain_two_grad)
     d_middle = cotangent + norm_back(back_two, middle, scale_two, gain_two)

time: 2140 us -> 2140 us (level)
    psum x1 -> x0, waiting for transfers between devices: 82.6 us -> none  [on_device(): lax.psum(through_weight(d_gate, full_gate) + through_weight(d_up, full_up...]
    all_gather x0 -> x1, waiting for transfers between devices: none -> 76.5 us  [on_device(): lax.all_gather(through_weight(d_gate, full_gate) + through_weight(d_up, f...]
where the time goes in v1:
time: 2140 us; the launch traced here: 2130 us
  waiting for transfers between devices  1620 us (76%)
  matrix products  241 us (11%)
  blocking collectives  158 us (7%)
  other arithmetic  55.8 us (3%)
  local copies, waits for them, and re-layouts  37.6 us (2%)
    reduce_scatter x1, waiting for transfers between devices, on_device(): lax.psum_scatter(down_sum, ('dp', 'seq'), scatter_dimension=1, tiled=True)  268 us
    reduce_scatter x1, waiting for transfers between devices, on_device(): lax.psum_scatter(up_sum, ('dp', 'seq'), scatter_dimension=0, tiled=True)  268 us
    reduce_scatter x1, waiting for transfers between devices, on_device(): lax.psum_scatter(gate_sum, ('dp', 'seq'), scatter_dimension=0, tiled=True)  268 us
    all_gather x1, waiting for transfers between devices, on_device(): lax.all_gather(w_gate, ('dp', 'seq'), axis=0, tiled=True)  104 us
    all_gather x1, waiting for transfers between devices, on_device(): lax.all_gather(w_down, ('dp', 'seq'), axis=1, tiled=True)  94.6 us
    all_gather x1, waiting for transfers between devices, on_device(): lax.all_gather(w_up, ('dp', 'seq'), axis=0, tiled=True)  94.1 us
    psum x1, waiting for transfers between devices, on_device(): middle = hidden + lax.psum(plain_dot(mixed, full_out), 'head')  79.8 us
    reduce_scatter x1, waiting for transfers between devices, on_device(): lax.psum_scatter(grad_out_w, ('dp', 'seq'), scatter_dimension=1, tiled=True)  79.2 us
  transfers between devices with their start and end apart: 18, of which 16 were waited for; matrix products, arithmetic and copies ran while one was open for 9% of the time, Pallas kernels for 0%

profile of v1, /device:TPU:0, one launch (start us, length us, event | category | flops | bytes accessed | tf_op | source)
XLA Modules:
  0.0 2130.8 jit_solution(3628382533721101746)
XLA Ops:
  8.7 38.7 %all_gather.40 = bf16[1536,128]{1,0:T(8,128)(2,1)S(1)} all-gather(bf16[96,128]{1,0:T(8,128)(2,1)} %param.31), channel_id=1, replica_groups=mesh['dp'=2,'seq'=8,'head'=2] {'dp','seq'}, dimensions={0}, use_global_device_ids=true | all-gather | bytes 417792 | tf_op jit(solution)/shard_map/all_gather | solution.py:93
  53.7 30.5 %all_gather.41 = bf16[1536,128]{1,0:T(8,128)(2,1)S(1)} all-gather(bf16[96,128]{1,0:T(8,128)(2,1)S(1)} %copy-done.40), channel_id=1, replica_groups=mesh['dp'=2,'seq'=8,'head'=2] {'dp','seq'}, dimensions={0}, use_global_device_ids=true | all-gather | bytes 417792 | tf_op jit(solution)/shard_map/all_gather | solution.py:94
  89.3 26.5 %all_gather.43 = s32[2,4,1024]{2,1,0:T(4,128)S(1)} all-gather(s32[2,4,128]{2,1,0:T(4,128)S(1)} %pad_add_fusion), channel_id=1, replica_groups=mesh['dp'=2,'seq'=8,'head'=2] {'seq'}, dimensions={2}, use_global_device_ids=true | all-gather | bytes 36864 | tf_op jit(solution)/shard_map/all_gather | solution.py:101
  115.8 4.7 convolution_add_fusion.3
  128.0 8.2 all-gather.9.cloned.1.call-done
  136.3 19.8 while.60
  137.0 4.8 fusion.176
  146.9 4.8 fusion.176
  156.1 10.1 while.61
  161.6 4.6 bitcast_add_fusion.6
  168.5 10.9 all-gather.13.cloned.1.call-done
  179.4 4.8 fusion.70
  189.1 79.8 %all-reduce.9.cloned.1.call-done = f32[512,1536]{1,0:T(8,128)} async-done(((f32[512,1536]{1,0:T(8,128)}), f32[512,1536]{1,0:T(8,128)}) %all-reduce.9.cloned.1.call-update) | async-done | bytes 3145744 | tf_op jit(solution)/shard_map/psum | solution.py:173
  274.4 104.3 %all-gather.15.cloned.1.call-done = bf16[1536,4480]{1,0:T(8,128)(2,1)} async-done(((bf16[96,4480]{1,0:T(8,128)(2,1)}), bf16[1536,4480]{1,0:T(8,128)(2,1)}) %all-gather.15.cloned.1.call-update) | async-done | bytes 13762576 | tf_op jit(solution)/shard_map/all_gather | solution.py:95
  378.7 13.4 fusion.107
  392.1 94.6 %all-gather.19.cloned.1.call-done = bf16[4480,1536]{0,1:T(8,128)(2,1)} async-done(((bf16[4480,96]{0,1:T(8,128)(2,1)}), bf16[4480,1536]{0,1:T(8,128)(2,1)}) %all-gather.19.cloned.1.call-update) | async-done | bytes 13762576 | tf_op jit(solution)/shard_map/all_gather | solution.py:98
  486.7 14.0 convolution_convert_fusion
  500.7 94.1 %all-gather.17.cloned.1.call-done = bf16[1536,4480]{1,0:T(8,128)(2,1)} async-done(((bf16[96,4480]{1,0:T(8,128)(2,1)}), bf16[1536,4480]{1,0:T(8,128)(2,1)}) %all-gather.17.cloned.1.call-update) | async-done | bytes 13762576 | tf_op jit(solution)/shard_map/all_gather | solution.py:96
  594.8 17.1 fusion.46
  614.0 11.9 fusion.108
  625.9 19.1 convolution_add_fusion.2
  647.2 76.5 %all-gather.21.cloned.1.call-done = f32[1024,1536]{1,0:T(8,128)} async-done(((f32[512,1536]{1,0:T(8,128)}), f32[1024,1536]{1,0:T(8,128)}) %all-gather.21.cloned.1.call-update) | async-done | bytes 6291472 | tf_op jit(solution)/shard_map/all_gather | solution.py:207
  723.7 5.4 reduce_sum.118
  740.2 20.2 while.62
  745.5 4.7 fusion.183
  751.1 4.6 fusion.182
  755.6 4.7 fusion.183
  762.9 38.9 %while.63 = (s32[]{:T(128)}, f32[4,128,6,128]{1,3,2,0:T(8,128)}, f32[4,1024,256]{1,2,0:T(8,128)}, bf16[4,1024,256]{2,1,0:T(8,128)(2,1)}, s32[4,128]{1,0:T(4,128)...) while((s32[]{:T(128)}, f32[4,128,6,128]{1,3,2,0:T(8,128)}, ...), condition=%wide.region_16.17_spmd.clone, body=%wide.region_15.16_spmd.clone.sunk | while | flops 2031091712 | bytes 71655744 | solution.py:257
  763.6 4.8 fusion.191
  768.5 5.3 fusion.192
  782.8 4.8 fusion.191
  787.6 5.3 fusion.192
  801.9 13.2 convolution_convert_fusion.1
  823.2 67.5 %reduce-scatter.14.cloned.1.call-done = f32[4,128,256]{1,2,0:T(8,128)} async-done(((f32[4,1024,256]{1,2,0:T(8,128)}), f32[4,128,256]{1,2,0:T(8,128)}) %reduce-scatter.14.cloned.1.call-update) | async-done | bytes 524304 | tf_op jit(solution)/shard_map/reduce_scatter | solution.py:266
  905.7 4.7 fusion.68
  916.1 15.0 fusion.111
  931.2 18.1 fusion.103
  950.7 15.2 fusion.112
  969.9 68.8 %all-reduce.11.cloned.1.call-done = (bf16[512,1536]{1,0:T(8,128)(2,1)}, bf16[512,1536]{1,0:T(8,128)(2,1)}) async-done(((bf16[512,1536]{1,0:T(8,128)(2,1)}, bf16[512,1536]{1,0:T(8,128)(2,1)}), (bf16[512,1536]{1,0:T(8,128)(2,1)}, bf16[512,1536]{1,0:T(8,128)(2,1)})) %all-reduce.11.cloned.1.call-update) | async-done | bytes 3145744 | tf_op jit(solution)/shard_map/psum | solution.py:182
  1041.7 62.7 %all-reduce.4 = (f32[1536]{0:T(1024)S(1)}, f32[6,128]{1,0:T(8,128)S(1)}, f32[1,128]{1,0:T(1,128)S(1)}, f32[1536]{0:T(1024)S(1)}) all-reduce(f32[1536]{0:T(1024)S(1)} %get-tuple-element.868, f32[6,128]{1,0:T(8,128)S(1)} %get-tuple-element.948, ...), channel_id=4, replica_groups=mesh['dp'=2,'seq'=8,'head'=2] {'dp','seq'}, use_global_device_ids=true, to_apply=%region_21.22.clone | all-reduce | flops 3968 | bytes 31744
  1106.9 5.1 fusion.53
  1112.0 7.3 reduce-scatter.16.cloned.1.call-done
  1119.3 79.2 %reduce-scatter.22.cloned.1.call-done = f32[768,96]{0,1:T(8,128)} async-done(((f32[768,1536]{0,1:T(8,128)}), f32[768,96]{0,1:T(8,128)}) %reduce-scatter.22.cloned.1.call-update) | async-done | bytes 294928 | tf_op jit(solution)/shard_map/reduce_scatter | solution.py:316
  1198.5 60.0 %reduce-scatter.18.cloned.1.call-done = f32[96,128]{1,0:T(8,128)} async-done(((f32[1536,128]{1,0:T(8,128)}), f32[96,128]{1,0:T(8,128)}) %reduce-scatter.18.cloned.1.call-update) | async-done | bytes 49168 | tf_op jit(solution)/shard_map/reduce_scatter | solution.py:314
  1258.5 59.8 %reduce-scatter.20.cloned.1.call-done = f32[96,128]{1,0:T(8,128)} async-done(((f32[1536,128]{1,0:T(8,128)}), f32[96,128]{1,0:T(8,128)}) %reduce-scatter.20.cloned.1.call-update) | async-done | bytes 49168 | tf_op jit(solution)/shard_map/reduce_scatter | solution.py:315
  1318.3 268.3 %reduce-scatter.24.cloned.1.call-done = f32[96,4480]{1,0:T(8,128)} async-done(((f32[1536,4480]{1,0:T(8,128)}), f32[96,4480]{1,0:T(8,128)}) %reduce-scatter.24.cloned.1.call-update) | async-done | bytes 1720336 | tf_op jit(solution)/shard_map/reduce_scatter | solution.py:321
  1586.6 268.4 %reduce-scatter.26.cloned.1.call-done = f32[96,4480]{1,0:T(8,128)} async-done(((f32[1536,4480]{1,0:T(8,128)}), f32[96,4480]{1,0:T(8,128)}) %reduce-scatter.26.cloned.1.call-update) | async-done | bytes 1720336 | tf_op jit(solution)/shard_map/reduce_scatter | solution.py:322
  1855.0 268.4 %reduce-scatter.28.cloned.1.call-done = f32[4480,96]{0,1:T(8,128)} async-done(((f32[4480,1536]{0,1:T(8,128)}), f32[4480,96]{0,1:T(8,128)}) %reduce-scatter.28.cloned.1.call-update) | async-done | bytes 1720336 | tf_op jit(solution)/shard_map/reduce_scatter | solution.py:323
  (265 shorter events, 128.8 us)
Async XLA Ops:
  7.2 43.4 %copy-start.5 = (bf16[4,128,1536]{2,1,0:T(8,128)(2,1)S(1)}, bf16[4,128,1536]{2,1,0:T(8,128)(2,1)}, u32[]{:S(2)}) copy-start(bf16[4,128,1536]{2,1,0:T(8,128)(2,1)} %param.24) | copy-start | bytes 4718596
  7.2 108.6 %all-gather.11.cloned.1.call-start = ((), (), s32[]{:S(2)}) async-start(), calls=%async_computation.10 | async-start | bytes 2506752 | tf_op jit(solution)/shard_map/all_gather | solution.py:92
  7.9 128.3 %all-gather.9.cloned.1.call-start = ((), (), s32[]{:S(2)}) async-start(), calls=%async_computation.9 | async-start | bytes 2359296 | tf_op jit(solution)/shard_map/all_gather | solution.py:123
  8.7 44.2 %copy-start.33 = (f32[1536]{0:T(1024)}, f32[1536]{0:T(1024)S(1)}, u32[]{:S(2)}) copy-start(f32[1536]{0:T(1024)S(1)} %convert_element_type.175) | copy-start | bytes 18436
  8.7 80.0 %copy-start.46 = (f32[64]{0:T(128)}, f32[64]{0:T(128)S(1)}, u32[]{:S(2)}) copy-start(f32[64]{0:T(128)S(1)} %multiply_power_fusion) | copy-start | bytes 772
  47.4 5.5 copy-start.19
  47.4 5.5 copy-start.30
  49.3 3.5 copy-start.41
  49.3 4.4 copy-start.40
  50.6 33.6 %copy-start.52 = (bf16[1,128]{1,0:T(2,128)(2,1)S(1)}, bf16[1,128]{1,0:T(2,128)(2,1)}, u32[]{:S(2)}) copy-start(bf16[1,128]{1,0:T(2,128)(2,1)} %param.34) | copy-start | bytes 772
  52.2 37.1 %copy-start.49 = (bf16[6,128]{1,0:T(8,128)(2,1)S(1)}, bf16[6,128]{1,0:T(8,128)(2,1)}, u32[]{:S(2)}) copy-start(bf16[6,128]{1,0:T(8,128)(2,1)} %param.30) | copy-start | bytes 4612
  52.2 37.1 %copy-start.31 = (s32[4,128]{1,0:T(4,128)S(1)}, s32[4,128]{1,0:T(4,128)}, u32[]{:S(2)}) copy-start(s32[4,128]{1,0:T(4,128)} %param.25) | copy-start | bytes 6148
  52.9 67.6 %copy-start.35 = (f32[512]{0:T(512)}, f32[512]{0:T(512)S(1)}, u32[]{:S(2)}) copy-start(f32[512]{0:T(512)S(1)} %convert_bitcast_fusion.1) | copy-start | bytes 6148
  87.8 91.5 %all-gather.13.cloned.1.call-start = ((), (), s32[]{:S(2)}) async-start(), calls=%async_computation.11 | async-start | bytes 2506752 | tf_op jit(solution)/shard_map/all_gather | solution.py:97
  88.6 180.3 %all-reduce.9.cloned.1.call-start = ((), (), s32[]{:S(2)}) async-start(), calls=%async_computation.12 | async-start | bytes 6291456 | tf_op jit(solution)/shard_map/psum | solution.py:173
  89.2 34.3 %copy-start.26 = (f32[512,64]{0,1:T(8,128)}, f32[512,64]{0,1:T(8,128)S(1)}, u32[]{:S(2)}) copy-start(f32[512,64]{0,1:T(8,128)S(1)} %get-tuple-element.976) | copy-start | bytes 393220
  89.2 34.3 %copy-start.28 = (f32[512,64]{0,1:T(8,128)}, f32[512,64]{0,1:T(8,128)S(1)}, u32[]{:S(2)}) copy-start(f32[512,64]{0,1:T(8,128)S(1)} %get-tuple-element.977) | copy-start | bytes 393220
  127.4 8.9 copy-start.15
  166.3 17.9 copy-start.43
  168.5 15.7 copy-start.17
  184.2 194.5 %all-gather.15.cloned.1.call-start = ((), (), s32[]{:S(2)}) async-start(), calls=%async_computation.13 | async-start | bytes 14622720 | tf_op jit(solution)/shard_map/all_gather | solution.py:95
  184.8 301.9 %all-gather.19.cloned.1.call-start = ((), (), s32[]{:S(2)}) async-start(), calls=%async_computation.15 | async-start | bytes 14622720 | tf_op jit(solution)/shard_map/all_gather | solution.py:98
  185.4 409.4 %all-gather.17.cloned.1.call-start = ((), (), s32[]{:S(2)}) async-start(), calls=%async_computation.14 | async-start | bytes 14622720 | tf_op jit(solution)/shard_map/all_gather | solution.py:96
  186.1 537.6 %all-gather.21.cloned.1.call-start = ((), (), s32[]{:S(2)}) async-start(), calls=%async_computation.24 | async-start | bytes 9437184 | tf_op jit(solution)/shard_map/all_gather | solution.py:207
  274.4 212.3 %copy-start.23 = (bf16[512,1536]{1,0:T(8,128)(2,1)S(1)}, bf16[512,1536]{1,0:T(8,128)(2,1)}, u32[]{:S(2)}) copy-start(bf16[512,1536]{1,0:T(8,128)(2,1)} %fusion.58) | copy-start | bytes 4718596
  645.0 245.7 %reduce-scatter.14.cloned.1.call-start = ((), (), s32[]{:S(2)}) async-start(), calls=%async_computation.16 | async-start | bytes 4718592 | tf_op jit(solution)/shard_map/reduce_scatter | solution.py:266
  723.7 9.8 copy-start.14
  729.1 4.4 copy-start.3
  729.1 4.7 copy-start.7
  768.5 7.6 copy-start
  787.6 7.6 copy-start
  801.9 166.6 %reduce-scatter.30.cloned.1.call-start = ((), (), s32[]{:S(2)}) async-start(), calls=%async_computation.25 | async-start | bytes 1114112
  801.9 13.2 copy-start.1
  820.0 71.9 %copy-start.36 = (f32[512]{0:T(512)S(1)}, f32[512]{0:T(512)}, u32[]{:S(2)}) copy-start(f32[512]{0:T(512)} %copy-done.35) | copy-start | bytes 6148
  820.0 71.9 %copy-start.47 = (f32[64]{0:T(128)S(1)}, f32[64]{0:T(128)}, u32[]{:S(2)}) copy-start(f32[64]{0:T(128)} %copy-done.46) | copy-start | bytes 772
  823.2 70.9 %copy-start.20 = (bf16[1536,128]{1,0:T(8,128)(2,1)S(1)}, bf16[1536,128]{1,0:T(8,128)(2,1)}, u32[]{:S(2)}) copy-start(bf16[1536,128]{1,0:T(8,128)(2,1)} %copy-done.19) | copy-start | bytes 1179652
  891.8 4.9 copy-start.18
  894.1 144.6 %all-reduce.11.cloned.1.call-start = ((), (), s32[]{:S(2)}) async-start(), calls=%async_computation.26 | async-start | bytes 6291456 | tf_op jit(solution)/shard_map/psum | solution.py:182
  898.5 220.8 %reduce-scatter.16.cloned.1.call-start = ((), (), s32[]{:S(2)}) async-start(), calls=%async_computation.17 | async-start | bytes 5013504 | tf_op jit(solution)/shard_map/reduce_scatter | solution.py:313
  903.8 294.7 %reduce-scatter.22.cloned.1.call-start = ((), (), s32[]{:S(2)}) async-start(), calls=%async_computation.20 | async-start | bytes 5013504 | tf_op jit(solution)/shard_map/reduce_scatter | solution.py:316
  910.4 348.1 %reduce-scatter.18.cloned.1.call-start = ((), (), s32[]{:S(2)}) async-start(), calls=%async_computation.18 | async-start | bytes 835584 | tf_op jit(solution)/shard_map/reduce_scatter | solution.py:314
  913.4 404.9 %reduce-scatter.20.cloned.1.call-start = ((), (), s32[]{:S(2)}) async-start(), calls=%async_computation.19 | async-start | bytes 835584 | tf_op jit(solution)/shard_map/reduce_scatter | solution.py:315
  916.0 670.6 %reduce-scatter.24.cloned.1.call-start = ((), (), s32[]{:S(2)}) async-start(), calls=%async_computation.21 | async-start | bytes 29245440 | tf_op jit(solution)/shard_map/reduce_scatter | solution.py:321
  931.1 923.9 %reduce-scatter.26.cloned.1.call-start = ((), (), s32[]{:S(2)}) async-start(), calls=%async_computation.22 | async-start | bytes 29245440 | tf_op jit(solution)/shard_map/reduce_scatter | solution.py:322
  949.3 1174.2 %reduce-scatter.28.cloned.1.call-start = ((), (), s32[]{:S(2)}) async-start(), calls=%async_computation.23 | async-start | bytes 29245440 | tf_op jit(solution)/shard_map/reduce_scatter | solution.py:323
  965.9 72.8 %copy-start.39 = (f32[512]{0:T(512)S(1)}, f32[512]{0:T(512)}, u32[]{:S(2)}) copy-start(f32[512]{0:T(512)} %copy-done.38) | copy-start | bytes 6148
  965.9 75.8 %copy-start.37 = (f32[1536]{0:T(1024)S(1)}, f32[1536]{0:T(1024)}, u32[]{:S(2)}) copy-start(f32[1536]{0:T(1024)} %get-tuple-element.866) | copy-start | bytes 18436
  965.9 141.0 %copy-start.4 = (f32[512,1536]{1,0:T(8,128)S(1)}, f32[512,1536]{1,0:T(8,128)}, u32[]{:S(2)}) copy-start(f32[512,1536]{1,0:T(8,128)} %copy-done.2) | copy-start | bytes 9437188
  (27 other events, 51.1 us)
Sparse Core Ops, SparseCore 0:
  10.2 45.8 all-gather.10
  88.0 48.2 all-gather.8
  138.5 40.8 all-gather.12
  184.3 84.5 all-reduce.8
  271.0 107.6 all-gather.14
  380.8 105.8 all-gather.18
  488.9 105.8 all-gather.16
  645.2 78.5 all-gather.20
  802.0 88.6 reduce-scatter.13
  894.2 57.3 reduce-scatter.29
  953.9 84.7 all-reduce.10
  1043.0 76.2 reduce-scatter.15
  1123.7 74.7 reduce-scatter.21
  1202.5 55.9 reduce-scatter.17
  1262.5 55.7 reduce-scatter.19
  1322.8 263.7 reduce-scatter.23
  1591.1 263.8 reduce-scatter.25
  1859.6 263.8 reduce-scatter.27
